TPU v7x, 8 devices: a whole 2x2x1 slice. The times are simulated.
8 devices in a mesh: dp: 2 (over z, y), pp: 4 (over x, core).
Axes of the slice: x: 2, y: 2, z: 1, core: 2. Of those that a mesh axis runs over, the one named last changes fastest.
Arguments:
- x: bfloat16 [8, 2048, 1024], P(None, 'dp')
- t: bfloat16 [8, 2048, 1024], P(None, 'dp')
- w1: bfloat16 [4, 2, 1024, 4096], P('pp')
- w2: bfloat16 [4, 2, 4096, 1024], P('pp')
Outputs:
- output 1: float32 [4, 2, 1024, 4096], P('pp')
- output 2: float32 [4, 2, 4096, 1024], P('pp')
- output 3: float32 [], replicated
All inputs are finite; a program needn't handle non-finite values.
Results may differ from a plain program's by a relative error of at most 0.00232167.
Values are sent between devices in bfloat16 or wider.
A program may use at most 1 GiB of HBM per device.

v0:
```python
import functools
import math
import jax
import jax.numpy as jnp
from jax import lax
from jax.experimental import pallas as pl
from jax.experimental.pallas import tpu as pltpu
from jax.sharding import PartitionSpec as P

MESH = pl.DeviceIdType.MESH
BF = jnp.bfloat16
F32 = jnp.float32
C = math.sqrt(2.0 / math.pi)
K3 = 0.044715
ROWS = 256
LAST_LAG = 4
BURST = 13
PAD = 256
SENDS = 4
PARTS = 4
KBLOCK = 1024
TILE1 = 512
TILE2 = 256
SLOTS = 4
DEPTH = 4


def _gelu(u):
    z = u * (C + (C * K3) * (u * u))
    return (0.5 * u) * (1.0 + jnp.tanh(z))


def _dgelu_and_gelu(u):
    u2 = u * u
    th = jnp.tanh(u * (C + (C * K3) * u2))
    half = 0.5 * (1.0 + th)
    d = half + (0.5 * u) * (1.0 - th * th) * (C + (3.0 * C * K3) * u2)
    return d, u * half


def _place(q):
    xx = q // 4
    s = (q // 2) % 2
    return ((s + xx) % 2, 2 * xx + q % 2)


def _kernel(inv, x, t, w1, w2,
            hb, ub, ab, eb, gb, tb, wb1, wb2, ls,
            w1v, w2v, av, hr, lacc, ho, hv, tv, gl, gv, go, uo, ui, ao, eo,
            s_wr, s_ws, s_h, s_g, s_t, s_hl, s_tl, s_gl, s_ul, s_uw, s_aw, s_ew, s_hs, s_gs, s_glw, s_px, s_l, s_lx, s_wl):
    units, rows, d = hb.shape
    half_units = units // 2
    ff = ub.shape[2]
    dp = lax.axis_index('dp')
    pp = lax.axis_index('pp')
    xx = pp // 2
    c = pp % 2
    s_in = (xx + dp) % 2
    p = 4 * xx + 2 * s_in + c
    first = p == 0
    last = p == 7
    holder = c == s_in
    nxt = _place(jnp.minimum(p + 1, 7))
    prv = _place(jnp.maximum(p - 1, 0))
    lag = LAST_LAG + 6 * (7 - p) + 2 * ((7 - p) // 2)

    barrier = pltpu.get_barrier_semaphore()
    for i in range(1, 8):
        pl.semaphore_signal(barrier, inc=1, device_id=_place((p + i) % 8), device_id_type=MESH)
    pl.semaphore_wait(barrier, 7)

    def cut(ref, n):
        return ref.at[:, pl.ds(0, n)]

    def remote(src, dst, ss, rs, to):
        return pltpu.make_async_remote_copy(src_ref=src, dst_ref=dst, send_sem=ss, recv_sem=rs,
                                            device_id=to, device_id_type=MESH)

    def local(src, dst, sem):
        return pltpu.make_async_copy(src, dst, sem)

    sib = (dp, 2 * xx + 1 - c)

    @pl.when(holder)
    def _():
        local(w1.at[c], cut(w1v, ff), s_wr.at[0]).start()
        local(w2.at[c], cut(w2v, d), s_wr.at[1]).start()
        remote(w1.at[1 - c], wb1, s_ws.at[0], s_wr.at[0], sib).start()
        remote(w2.at[1 - c], wb2, s_ws.at[1], s_wr.at[1], sib).start()

    def push(src, dst, base, sem, to, k):
        remote(src.at[k], dst.at[base + k], s_px, sem.at[base + k], to).start()

    def push_all(src, dst, base, sem, to, n):
        def step(k, carry):
            push(src, dst, base, sem, to, k)
            return carry
        lax.fori_loop(0, n, step, 0)

    @pl.when(p == 1)
    def _():
        push_all(x, hb, 0, s_h, _place(0), half_units)

    @pl.when(p == 3)
    def _():
        push_all(x, hb, half_units, s_h, _place(0), half_units)

    @pl.when(p == 6)
    def _():
        push_all(t, tb, 0, s_t, _place(7), half_units)

    @pl.when(p == 4)
    def _():
        push_all(t, tb, half_units, s_t, _place(7), BURST)

    def paced_push(m):
        j = BURST + m // 2

        @pl.when((p == 4) & (j < half_units))
        def _():
            push(t, tb, half_units, s_t, _place(7), j)

    lacc[...] = jnp.zeros_like(lacc)
    local(w1.at[c], cut(w1v, ff), s_wr.at[0]).wait()

    @pl.when(jnp.logical_not(holder))
    def _():
        local(wb1, cut(w1v, ff), s_wl.at[0]).start()
    local(w2.at[c], cut(w2v, d), s_wr.at[1]).wait()

    @pl.when(jnp.logical_not(holder))
    def _():
        local(wb2, cut(w2v, d), s_wl.at[1]).start()
        local(wb1, cut(w1v, ff), s_wl.at[0]).wait()
        local(wb2, cut(w2v, d), s_wl.at[1]).wait()

    nt = (((1,), (1,)), ((), ()))
    nc, no = ff // PARTS, d // PARTS

    def f1(s, j):
        sl, so = slice(j * nc, (j + 1) * nc), slice(j * no, (j + 1) * no)
        u = jnp.dot(hv[s, :, :d], w1v[:, sl], preferred_element_type=F32).astype(BF)
        uo[s, :, sl] = u
        av[:, sl] = _gelu(u.astype(F32)).astype(BF)
        hr[:, so] = hv[s, :, so]

    def f2(k, s, j):
        sl = slice(j * no, (j + 1) * no)
        acc = jnp.dot(av[:, :ff], w2v[:, sl], preferred_element_type=F32)
        y = (hr[:, sl].astype(F32) + acc).astype(BF)
        ho[k % SENDS, :, sl] = y
        r = y.astype(F32) - tv[s, :, sl].astype(F32)
        gl[s, :, sl] = (r * inv).astype(BF)
        lacc[:, sl] += jnp.sum((r * r).reshape(rows // 8, 8, no), axis=0)

    def b1(s, j):
        sl = slice(j * nc, (j + 1) * nc)
        q = lax.dot_general(gv[s, :, :d], w2v[sl, :d], nt, preferred_element_type=F32)
        dg, a = _dgelu_and_gelu(ui[s, :, sl].astype(F32))
        ao[s, :, sl] = a.astype(BF)
        eo[s, :, sl] = (dg * q).astype(BF)

    def b2(s, j):
        sl = slice(j * no, (j + 1) * no)
        acc = lax.dot_general(eo[s, :, :ff], w1v[sl, :ff], nt, preferred_element_type=F32)
        go[s, :, sl] = (gv[s, :, sl].astype(F32) + acc).astype(BF)

    def h_load(k, s):
        return local(hb.at[k], cut(hv.at[s], d), s_hl.at[s])

    def t_load(k, s):
        return local(tb.at[k], cut(tv.at[s], d), s_tl.at[s])

    def g_load(m, s):
        return local(gb.at[m], cut(gv.at[s], d), s_gl.at[s])

    def u_load(m, s):
        return local(ub.at[m], cut(ui.at[s], ff), s_ul.at[s])

    def u_write(k, s):
        return local(cut(uo.at[s], ff), ub.at[k], s_uw.at[s])

    def a_write(m, s):
        return local(cut(ao.at[s], ff), ab.at[m], s_aw.at[s])

    def e_write(m, s):
        return local(cut(eo.at[s], ff), eb.at[m], s_ew.at[s])

    def gl_write(k, s):
        return local(cut(gl.at[s], d), gb.at[k], s_glw.at[s])

    def h_send(k, s):
        return remote(ho.at[k % SENDS, :, pl.ds(0, d)], hb.at[k], s_hs.at[k % SENDS], s_h.at[k], nxt)

    def g_send(m, s):
        return remote(cut(go.at[s], d), gb.at[m], s_gs.at[s], s_g.at[m], prv)

    def fetch_h(k, s):
        local(hb.at[k], hb.at[k], s_h.at[k]).wait()
        h_load(k, s).start()

    def fetch_t(k, s):
        @pl.when(last)
        def _():
            local(tb.at[k], tb.at[k], s_t.at[k]).wait()
            t_load(k, s).start()

    def fetch_g(m, s):
        @pl.when(jnp.logical_not(last))
        def _():
            local(gb.at[m], gb.at[m], s_g.at[m]).wait()
        g_load(m, s).start()

    def wait_t(k, s):
        @pl.when(last)
        def _():
            t_load(k, s).wait()

    def wait_gl(k, s):
        @pl.when(last & (k >= 0))
        def _():
            gl_write(k, s).wait()

    def wait_h_send(k, s):
        @pl.when(jnp.logical_not(last) & (k >= 0))
        def _():
            h_send(k, s).wait_send()

    def wait_b_outputs(m, s):
        a_write(m, s).wait()
        e_write(m, s).wait()

        @pl.when(p > 0)
        def _():
            g_send(m, s).wait_send()

    def put_f(k, s):
        @pl.when(last)
        def _():
            gl_write(k, s).start()

        @pl.when(jnp.logical_not(last))
        def _():
            h_send(k, s).start()

    def put_b(m, s):
        @pl.when(p > 0)
        def _():
            g_send(m, s).start()

    def warm(k, carry):
        s = k % 2
        h_load(k, s).wait()
        wait_t(k, s)

        @pl.when(k >= 2)
        def _():
            u_write(k - 2, s).wait()
        wait_gl(k - 2, s)
        wait_h_send(k - SENDS, s)
        for j in range(PARTS):
            f1(s, j)
        for j in range(PARTS):
            f2(k, s, j)
        put_f(k, s)
        u_write(k, s).start()
        fetch_h(k + 1, 1 - s)
        fetch_t(k + 1, 1 - s)
        return carry

    def steady(i, carry):
        for s in (0, 1):
            m = 2 * i + s
            k = lag + m
            if s == 0:
                paced_push(m)
            h_load(k, s).wait()
            wait_t(k - 1, 1 - s)
            g_load(m, s).wait()
            u_load(m, s).wait()
            u_write(k - 2, s).wait()
            wait_gl(k - 3, 1 - s)
            wait_h_send(k - 1 - SENDS, 1 - s)

            @pl.when(m >= 2)
            def _():
                wait_b_outputs(m - 2, s)
            u_load(m + 1, 1 - s).start()

            @pl.when(k + 1 < units)
            def _():
                fetch_h(k + 1, 1 - s)
            fetch_t(k, s)
            fetch_g(m + 1, 1 - s)
            for j in range(PARTS):
                f2(k - 1, 1 - s, j)
                b1(s, j)
            for j in range(PARTS):
                b2(s, j)
                f1(s, j)
            put_f(k - 1, 1 - s)
            put_b(m, s)
            u_write(k, s).start()
            e_write(m, s).start()
            a_write(m, s).start()
        return carry

    def cool(i, carry):
        m = units - lag + i
        s = m % 2
        g_load(m, s).wait()
        u_load(m, s).wait()

        @pl.when(m >= 2)
        def _():
            wait_b_outputs(m - 2, s)

        @pl.when(m + 1 < units)
        def _():
            u_load(m + 1, 1 - s).start()
        for j in range(PARTS):
            b1(s, j)
        for j in range(PARTS):
            b2(s, j)
        put_b(m, s)
        e_write(m, s).start()
        a_write(m, s).start()

        @pl.when(m + 1 < units)
        def _():
            fetch_g(m + 1, 1 - s)
        return carry

    fetch_h(0, 0)
    fetch_t(0, 0)
    lax.fori_loop(0, lag - 1, warm, 0)

    h_load(lag - 1, 1).wait()
    u_write(lag - 3, 1).wait()
    for j in range(PARTS):
        f1(1, j)
    u_write(lag - 1, 1).start()
    fetch_h(lag, 0)
    u_load(0, 0).start()
    fetch_g(0, 0)
    lax.fori_loop(0, (units - lag) // 2, steady, 0)

    wait_t(units - 1, 1)
    wait_gl(units - 3, 1)
    wait_h_send(units - 1 - SENDS, 1)
    for j in range(PARTS):
        f2(units - 1, 1, j)
    put_f(units - 1, 1)
    u_write(units - 2, 0).wait()
    u_write(units - 1, 1).wait()
    wait_gl(units - 2, 0)
    wait_gl(units - 1, 1)

    @pl.when(last)
    def _():
        local(lacc, ls, s_l).start()
        for i in range(7):
            remote(lacc, ls, s_lx.at[i], s_l, _place(i)).start()

    lax.fori_loop(0, lag, cool, 0)
    for i in range(SENDS):
        wait_h_send(units - SENDS + i, i % 2)
    wait_b_outputs(units - 2, 0)
    wait_b_outputs(units - 1, 1)
    local(lacc, ls, s_l).wait()

    @pl.when(last)
    def _():
        for i in range(7):
            remote(lacc, ls, s_lx.at[i], s_l, _place(i)).wait_send()

    @pl.when(holder)
    def _():
        remote(w1.at[1 - c], wb1, s_ws.at[0], s_wr.at[0], sib).wait_send()
        remote(w2.at[1 - c], wb2, s_ws.at[1], s_wr.at[1], sib).wait_send()

    @pl.when((p == 1) | (p == 3))
    def _():
        remote(x, hb.at[pl.ds(0, half_units)], s_px, s_h.at[0], _place(0)).wait_send()

    @pl.when((p == 4) | (p == 6))
    def _():
        remote(t, tb.at[pl.ds(0, half_units)], s_px, s_t.at[0], _place(7)).wait_send()


def _forward_backward(x, t, w1, w2, inv):
    half_units, rows, d = x.shape
    units = 2 * half_units
    ff = w1.shape[-1]
    any_ = pl.BlockSpec(memory_space=pl.ANY)
    dw, fw = d + PAD, ff + PAD
    small = [pltpu.VMEM((2, rows, dw), BF)]
    big = [pltpu.VMEM((2, rows, fw), BF)]
    dma = pltpu.SemaphoreType.DMA
    narrow = jax.ShapeDtypeStruct((units, rows, d), BF)
    wide = jax.ShapeDtypeStruct((units, rows, ff), BF)

    def kern(*refs):
        _kernel(inv, *refs)

    flops = 8 * units * rows * d * ff
    return pl.pallas_call(
        kern,
        out_shape=(narrow, wide, wide, wide, narrow, narrow, jax.ShapeDtypeStruct((d, ff), BF),
                   jax.ShapeDtypeStruct((ff, d), BF), jax.ShapeDtypeStruct((8, d), F32)),
        in_specs=[any_] * 4,
        out_specs=[any_] * 9,
        scratch_shapes=[
            pltpu.VMEM((d, fw), BF), pltpu.VMEM((ff, dw), BF), pltpu.VMEM((rows, fw), BF),
            pltpu.VMEM((rows, dw), BF), pltpu.VMEM((8, d), F32), pltpu.VMEM((SENDS, rows, dw), BF),
            *(small * 5), *(big * 4),
            dma((2,)), dma((2,)), dma((units,)), dma((units,)), dma((units,)),
            dma((2,)), dma((2,)), dma((2,)), dma((2,)), dma((2,)), dma((2,)), dma((2,)),
            dma((SENDS,)), dma((2,)), dma((2,)), dma(()), dma(()), dma((7,)), dma((2,)),
        ],
        compiler_params=pltpu.CompilerParams(collective_id=0, has_side_effects=True, vmem_limit_bytes=67043328),
        cost_estimate=pl.CostEstimate(flops=flops, bytes_accessed=10 * units * rows * ff, transcendentals=0),
    )(x, t, w1, w2)


def _grad_kernel(h, e, a, g, dw1, dw2, rest, narrow, wide1, wide2, acc1, acc2, s_n, s_w, s_keep, s_send, s_in):
    tokens, d = h.shape
    ff = e.shape[1]
    blocks = tokens // KBLOCK
    dp = lax.axis_index('dp')
    pp = lax.axis_index('pp')
    xx = pp // 2
    c = pp % 2
    side = (xx + dp) % 2
    own = c == side
    here = (dp, 2 * xx + side)
    there = (1 - dp, 2 * xx + side)

    barrier = pltpu.get_barrier_semaphore()
    for i in range(1, 4):
        to = ((dp + i // 2) % 2, 2 * xx + (c + i) % 2)
        pl.semaphore_signal(barrier, inc=1, device_id=to, device_id_type=MESH)
    pl.semaphore_wait(barrier, 3)

    def phase(thin, fat, wide, acc, out, cols, arr):
        tile = wide.shape[-1]
        tiles = ff // tile
        sent = tiles - 1 if cols else tiles

        def load(t, s):
            k = pl.multiple_of((t % blocks) * KBLOCK, KBLOCK)
            n = pl.multiple_of((t // blocks) * tile, tile)
            return (pltpu.make_async_copy(thin.at[pl.ds(k, KBLOCK)], narrow.at[s], s_n.at[s]),
                    pltpu.make_async_copy(fat.at[pl.ds(k, KBLOCK), pl.ds(n, tile)], wide.at[s], s_w.at[s]))

        def place(i):
            n = pl.multiple_of(i * tile, tile)
            return out.at[c, :, pl.ds(n, tile)] if cols else out.at[c, pl.ds(n, tile)]

        def keep_local(i, slot):
            return pltpu.make_async_copy(acc.at[slot], place(i), s_keep.at[arr, slot])

        def keep_remote(i, slot):
            return pltpu.make_async_remote_copy(acc.at[slot], place(i), s_keep.at[arr, slot], s_in.at[arr, c],
                                                device_id=here, device_id_type=MESH)

        def send(i, slot):
            return pltpu.make_async_remote_copy(acc.at[slot], place(i), s_send.at[arr, slot], s_in.at[arr, c],
                                                device_id=there, device_id_type=MESH)

        def rest_local(slot):
            return pltpu.make_async_copy(acc.at[slot], rest, s_keep.at[arr, slot])

        def drain(i, slot):
            send(i, slot).wait_send()

            @pl.when(jnp.logical_not(own))
            def _():
                keep_remote(i, slot).wait_send()

            @pl.when(own)
            def _():
                keep_local(i, slot).wait()

        for ahead in range(DEPTH - 1):
            for cp in load(ahead, ahead):
                cp.start()

        def step(t, carry):
            s = t % DEPTH
            i = t // blocks
            k = t % blocks
            slot = i % SLOTS

            @pl.when(k == 0)
            def _():
                @pl.when(i >= SLOTS)
                def _():
                    drain(i - SLOTS, slot)
                acc[slot] = jnp.zeros(acc.shape[1:], F32)
            for cp in load(t, s):
                cp.wait()

            @pl.when(t + DEPTH - 1 < tiles * blocks)
            def _():
                for cp in load(t + DEPTH - 1, (t + DEPTH - 1) % DEPTH):
                    cp.start()
            lhs, rhs = (narrow, wide) if cols else (wide, narrow)
            for q in range(acc.shape[1] // 256):
                rows = slice(q * 256, (q + 1) * 256)
                acc[slot, rows, :] += lax.dot_general(lhs[s, :, rows], rhs[s], (((0,), (0,)), ((), ())),
                                                      preferred_element_type=F32)

            if sent < tiles:
                @pl.when(t == tiles * blocks - 1)
                def _():
                    rest_local(slot).start()

            @pl.when((k == blocks - 1) & (i < sent))
            def _():
                send(i, slot).start()

                @pl.when(own)
                def _():
                    keep_local(i, slot).start()

                @pl.when(jnp.logical_not(own))
                def _():
                    keep_remote(i, slot).start()
            return carry

        lax.fori_loop(0, tiles * blocks, step, 0)
        for i in range(tiles - SLOTS, sent):
            late.append(functools.partial(drain, i, i % SLOTS))
        if sent < tiles:
            late.append(lambda: rest_local((tiles - 1) % SLOTS).wait())

    late = []
    phase(g, a, wide2, acc2, dw2, False, 1)
    phase(h, e, wide1, acc1, dw1, True, 0)
    for wait in late:
        wait()

    for j in (0, 1):
        @pl.when(jnp.logical_not(own) | (c != j))
        def _():
            part = dw1.at[j, :, pl.ds(0, ff - TILE1)]
            pltpu.make_async_copy(part, part, s_in.at[0, j]).wait()
            pltpu.make_async_copy(dw2.at[j], dw2.at[j], s_in.at[1, j]).wait()


def _gradients(h, e, a, g):
    tokens, d = h.shape
    ff = e.shape[1]
    any_ = pl.BlockSpec(memory_space=pl.ANY)
    dma = pltpu.SemaphoreType.DMA
    return pl.pallas_call(
        _grad_kernel,
        out_shape=(jax.ShapeDtypeStruct((2, d, ff), F32), jax.ShapeDtypeStruct((2, ff, d), F32),
                   jax.ShapeDtypeStruct((d, TILE1), F32)),
        in_specs=[any_] * 4,
        out_specs=[any_] * 3,
        scratch_shapes=[
            pltpu.VMEM((DEPTH, KBLOCK, d), BF), pltpu.VMEM((DEPTH, KBLOCK, TILE1), BF),
            pltpu.VMEM((DEPTH, KBLOCK, TILE2), BF), pltpu.VMEM((SLOTS, d, TILE1), F32), pltpu.VMEM((SLOTS, TILE2, d), F32),
            dma((DEPTH,)), dma((DEPTH,)), dma((2, SLOTS)), dma((2, SLOTS)), dma((2, 2)),
        ],
        compiler_params=pltpu.CompilerParams(collective_id=1, has_side_effects=True, vmem_limit_bytes=67043328),
        cost_estimate=pl.CostEstimate(flops=4 * tokens * d * ff, bytes_accessed=4 * tokens * ff, transcendentals=0),
    )(h, e, a, g)


def _copy_kernel(a, b, a_out, b_out):
    a_out[...] = a[...]
    b_out[...] = b[...]


def _copies(dw1, dw2):
    _, d, ff = dw1.shape
    specs = [pl.BlockSpec((1, d // 8, ff), lambda j, i: (j, i, 0)), pl.BlockSpec((1, ff // 8, d), lambda j, i: (j, i, 0))]
    return pl.pallas_call(
        _copy_kernel,
        grid=(2, 8),
        out_shape=(jax.ShapeDtypeStruct(dw1.shape, F32), jax.ShapeDtypeStruct(dw2.shape, F32)),
        in_specs=specs,
        out_specs=specs,
        cost_estimate=pl.CostEstimate(flops=10 ** 11, bytes_accessed=32 * d * ff, transcendentals=0),
    )(dw1, dw2)


def solution(mesh):
    def flat(x, y, c):
        return y * 4 + 2 * x + c

    chips = [(x, y) for x in (0, 1) for y in (0, 1)]
    keep = [[(flat(x, y, j), flat(x, y, 1 - j)) for x, y in chips if (x + y) % 2 != j] for j in (0, 1)]
    swap = [[(flat(x, y, j), flat(x, 1 - y, (x + y) % 2)) for x, y in chips] for j in (0, 1)]

    def body(x, t, w1, w2):
        nm, tok, d = x.shape
        ff = w1.shape[-1]
        inv = 1.0 / (nm * tok * mesh.shape['dp'] * d)
        xs = x.reshape(nm * tok // ROWS, ROWS, d)
        ts = t.reshape(nm * tok // ROWS, ROWS, d)
        hb, _, ab, eb, gb, _, _, _, ls = _forward_backward(xs, ts, w1[0], w2[0], inv)
        n = hb.shape[0] * ROWS
        dw1, dw2, rest = _gradients(hb.reshape(n, d), eb.reshape(n, ff), ab.reshape(n, ff), gb.reshape(n, d))
        pp = lax.axis_index('pp')
        own = (pp // 2 + lax.axis_index('dp')) % 2 == pp % 2
        there = [lax.ppermute(rest, ('dp', 'pp'), swap[j]) for j in (0, 1)]
        here = [lax.ppermute(rest, ('dp', 'pp'), keep[j]) for j in (0, 1)]
        dw1, dw2 = _copies(dw1, dw2)
        for j in (0, 1):
            part = jnp.where(own, jnp.where(pp % 2 == j, rest, here[j]), there[j])
            dw1 = lax.dynamic_update_slice(dw1, part[None], (j, 0, ff - TILE1))
        loss = 0.5 * inv * jnp.sum(ls)
        return dw1[None], dw2[None], loss

    return jax.shard_map(body, mesh=mesh,
                         in_specs=(P(None, 'dp', None), P(None, 'dp', None), P('pp'), P('pp')),
                         out_specs=(P('pp'), P('pp'), P()), check_vma=False)
```

profile of v0, /device:TPU:1, one launch (start us, length us, event | category | flops | bytes accessed | tf_op | source)
XLA Modules:
  0.0 1585.6 jit_solution(5827855748928248127)
XLA Ops:
  0.6 818.1 %shard_map.67 = (bf16[64,256,1024]{2,1,0:T(8,128)(2,1)}, bf16[64,256,4096]{2,1,0:T(8,128)(2,1)}, bf16[64,256,4096]{2,1,0:T(8,128)(2,1)}, bf16[64,256,4096]{2,1,0...) custom-call(bf16[32,256,1024]{2,1,0:T(8,128)(2,1)} %bitcast.15, ...), custom_call_target="tpu_custom_call" | custom-call | flops 549755813888 | bytes 671088640 | tf_op jit(solution)/shard_map/pallas_call | solution.py:407
  818.8 699.7 %shard_map.68 = (f32[2,1024,4096]{2,1,0:T(8,128)}, f32[2,4096,1024]{2,1,0:T(8,128)}, f32[1024,512]{1,0:T(8,128)}) custom-call(bf16[16384,1024]{1,0:T(8,128)(2,1)} %bitcast.20, bf16[16384,4096]{1,0:T(8,128)(2,1)} %bitcast.5.e, bf16[16384,4096]{1,0:T(8,128)(2,1)} %bitcast.6.a, bf16[16384,1024]{1,0:T(8,128)(2,1)} %bitcast.21), custom_call_target="tpu_custom_call" | custom-call | flops 274877906944 | bytes 268435456 | tf_op jit(solution)/shard_map/pallas_call | solution.py:557
  1518.5 1.3 collective-permute-start.1
  1519.8 2.0 collective-permute-start
  1521.8 4.9 collective-permute-start.3
  1526.7 3.3 collective-permute-start.2
  1530.0 0.0 copy-start.1
  1530.0 0.0 copy-start
  1530.0 45.2 %shard_map.69 = (f32[2,1024,4096]{2,1,0:T(8,128)}, f32[2,4096,1024]{2,1,0:T(8,128)}) custom-call(f32[2,1024,4096]{2,1,0:T(8,128)} %get-tuple-element.17.a, f32[2,4096,1024]{2,1,0:T(8,128)} %get-tuple-element.18.b), custom_call_target="tpu_custom_call" | custom-call | flops 99999997952 | bytes 134217728 | tf_op jit(solution)/shard_map/pallas_call | solution.py:581
  1575.2 0.0 copy-done.1
  1575.2 0.6 reduce_sum.9
  1576.5 0.0 collective-permute-done.1
  1576.5 0.0 collective-permute-done
  1576.5 0.0 copy-done
  1576.5 4.3 bitcast_dynamic-update-slice_fusion.1
  1580.8 0.0 collective-permute-done.3
  1580.8 0.0 collective-permute-done.2
  1580.8 3.7 bitcast_dynamic-update-slice_fusion
Async XLA Ops:
  1518.5 58.0 %collective-permute-start.1 = (f32[1024,512]{1,0:T(8,128)}, f32[1024,512]{1,0:T(8,128)}, u32[]{:S(2)}, u32[]{:S(2)}) collective-permute-start(f32[1024,512]{1,0:T(8,128)} %get-tuple-element.20), channel_id=1, source_target_pairs={{0,4},{4,1},{2,7},{6,2}} | collective-permute-start | bytes 6291464 | tf_op jit(solution)/shard_map/ppermute | solution.py:610
  1519.8 56.7 %collective-permute-start = (f32[1024,512]{1,0:T(8,128)}, f32[1024,512]{1,0:T(8,128)}, u32[]{:S(2)}, u32[]{:S(2)}) collective-permute-start(f32[1024,512]{1,0:T(8,128)} %get-tuple-element.20), channel_id=1, source_target_pairs={{4,5},{2,3}} | collective-permute-start | bytes 6291464 | tf_op jit(solution)/shard_map/ppermute | solution.py:611
  1521.8 59.0 %collective-permute-start.3 = (f32[1024,512]{1,0:T(8,128)}, f32[1024,512]{1,0:T(8,128)}, u32[]{:S(2)}, u32[]{:S(2)}) collective-permute-start(f32[1024,512]{1,0:T(8,128)} %get-tuple-element.20), channel_id=1, source_target_pairs={{1,4},{5,1},{3,7},{7,2}} | collective-permute-start | bytes 6291464 | tf_op jit(solution)/shard_map/ppermute | solution.py:610
  1526.7 54.1 %collective-permute-start.2 = (f32[1024,512]{1,0:T(8,128)}, f32[1024,512]{1,0:T(8,128)}, u32[]{:S(2)}, u32[]{:S(2)}) collective-permute-start(f32[1024,512]{1,0:T(8,128)} %get-tuple-element.20), channel_id=1, source_target_pairs={{1,0},{7,6}} | collective-permute-start | bytes 6291464 | tf_op jit(solution)/shard_map/ppermute | solution.py:611
  1530.0 45.2 %copy-start.1 = (f32[8,1024]{1,0:T(8,128)S(1)}, f32[8,1024]{1,0:T(8,128)}, u32[]{:S(2)}) copy-start(f32[8,1024]{1,0:T(8,128)} %get-tuple-element.22) | copy-start | bytes 98308
  1530.0 46.5 %copy-start = (f32[1024,512]{1,0:T(8,128)S(1)}, f32[1024,512]{1,0:T(8,128)}, u32[]{:S(2)}) copy-start(f32[1024,512]{1,0:T(8,128)} %get-tuple-element.20) | copy-start | bytes 6291460
where the time goes:
time: 1590 us
  Pallas kernels  1560 us (98%)
    pallas_call x1, Pallas kernels, _forward_backward(): pl.pallas_call(kern, out_shape=(narrow, wide, wide, wide, narrow, narrow,...  818 us
    pallas_call x1, Pallas kernels, _gradients(): pl.pallas_call(_grad_kernel, out_shape=(jax.ShapeDtypeStruct((2, d, ff),...  700 us
    pallas_call x1, Pallas kernels, _copies(): pl.pallas_call(_copy_kernel, grid=(2, 8), out_shape=(jax.ShapeDtypeStruct...  45.2 us
  transfers between devices with their start and end apart: 4, of which 0 were waited for; matrix products, arithmetic and copies ran while one was open for 0% of the time, Pallas kernels for 3%

commit v1 on v0

--- a/solution.py
+++ b/solution.py
@@ -22,6 +22,7 @@
 TILE1 = 512
 TILE2 = 256
 SLOTS = 4
+DETOUR = 5
 DEPTH = 4
 
 
@@ -423,7 +424,8 @@
     )(x, t, w1, w2)
 
 
-def _grad_kernel(h, e, a, g, dw1, dw2, rest, narrow, wide1, wide2, acc1, acc2, s_n, s_w, s_keep, s_send, s_in):
+def _grad_kernel(h, e, a, g, dw1, dw2, rest, via1, via2, narrow, wide1, wide2, acc1, acc2,
+                 s_n, s_w, s_keep, s_send, s_in, s_via, s_relay):
     tokens, d = h.shape
     ff = e.shape[1]
     blocks = tokens // KBLOCK
@@ -440,7 +442,14 @@
     for i in range(1, 4):
         to = ((dp + i // 2) % 2, 2 * xx + (c + i) % 2)
         pl.semaphore_signal(barrier, inc=1, device_id=to, device_id_type=MESH)
-    pl.semaphore_wait(barrier, 3)
+    @pl.when(xx == 1)
+    def _():
+        pl.semaphore_signal(barrier, inc=1, device_id=(dp, c), device_id_type=MESH)
+        pl.semaphore_wait(barrier, 3)
+
+    @pl.when(xx == 0)
+    def _():
+        pl.semaphore_wait(barrier, 4)
 
     def phase(thin, fat, wide, acc, out, cols, arr):
         tile = wide.shape[-1]
@@ -467,6 +476,10 @@
         def send(i, slot):
             return pltpu.make_async_remote_copy(acc.at[slot], place(i), s_send.at[arr, slot], s_in.at[arr, c],
                                                 device_id=there, device_id_type=MESH)
+
+        def detour(slot):
+            return pltpu.make_async_remote_copy(acc.at[slot], via1, s_send.at[arr, slot], s_via.at[0],
+                                                device_id=(dp, 2 + c), device_id_type=MESH)
 
         def rest_local(slot):
             return pltpu.make_async_copy(acc.at[slot], rest, s_keep.at[arr, slot])
@@ -518,7 +531,18 @@
 
             @pl.when((k == blocks - 1) & (i < sent))
             def _():
-                send(i, slot).start()
+                if cols:
+                    send(i, slot).start()
+                else:
+                    around = (xx == 0) & (i == DETOUR)
+
+                    @pl.when(jnp.logical_not(around))
+                    def _():
+                        send(i, slot).start()
+
+                    @pl.when(around)
+                    def _():
+                        detour(slot).start()
 
                 @pl.when(own)
                 def _():
@@ -536,10 +560,29 @@
             late.append(lambda: rest_local((tiles - 1) % SLOTS).wait())
 
     late = []
+    relay1 = pltpu.make_async_remote_copy(via1, via2, s_relay.at[0], s_via.at[1],
+                                          device_id=(1 - dp, 2 + c), device_id_type=MESH)
+    relay2 = pltpu.make_async_remote_copy(via2, dw2.at[c, pl.ds(DETOUR * TILE2, TILE2)], s_relay.at[1], s_in.at[1, c],
+                                          device_id=(dp, 1 - dp), device_id_type=MESH)
     phase(g, a, wide2, acc2, dw2, False, 1)
+
+    @pl.when(xx == 1)
+    def _():
+        pltpu.make_async_copy(via1, via1, s_via.at[0]).wait()
+        relay1.start()
     phase(h, e, wide1, acc1, dw1, True, 0)
+
+    @pl.when(xx == 1)
+    def _():
+        pltpu.make_async_copy(via2, via2, s_via.at[1]).wait()
+        relay2.start()
     for wait in late:
         wait()
+
+    @pl.when(xx == 1)
+    def _():
+        relay1.wait_send()
+        relay2.wait_send()
 
     for j in (0, 1):
         @pl.when(jnp.logical_not(own) | (c != j))
@@ -557,13 +600,14 @@
     return pl.pallas_call(
         _grad_kernel,
         out_shape=(jax.ShapeDtypeStruct((2, d, ff), F32), jax.ShapeDtypeStruct((2, ff, d), F32),
-                   jax.ShapeDtypeStruct((d, TILE1), F32)),
+                   jax.ShapeDtypeStruct((d, TILE1), F32),
+                   jax.ShapeDtypeStruct((TILE2, d), F32), jax.ShapeDtypeStruct((TILE2, d), F32)),
         in_specs=[any_] * 4,
-        out_specs=[any_] * 3,
+        out_specs=[any_] * 5,
         scratch_shapes=[
             pltpu.VMEM((DEPTH, KBLOCK, d), BF), pltpu.VMEM((DEPTH, KBLOCK, TILE1), BF),
             pltpu.VMEM((DEPTH, KBLOCK, TILE2), BF), pltpu.VMEM((SLOTS, d, TILE1), F32), pltpu.VMEM((SLOTS, TILE2, d), F32),
-            dma((DEPTH,)), dma((DEPTH,)), dma((2, SLOTS)), dma((2, SLOTS)), dma((2, 2)),
+            dma((DEPTH,)), dma((DEPTH,)), dma((2, SLOTS)), dma((2, SLOTS)), dma((2, 2)), dma((2,)), dma((2,)),
         ],
         compiler_params=pltpu.CompilerParams(collective_id=1, has_side_effects=True, vmem_limit_bytes=67043328),
         cost_estimate=pl.CostEstimate(flops=4 * tokens * d * ff, bytes_accessed=4 * tokens * ff, transcendentals=0),
@@ -604,7 +648,7 @@
         ts = t.reshape(nm * tok // ROWS, ROWS, d)
         hb, _, ab, eb, gb, _, _, _, ls = _forward_backward(xs, ts, w1[0], w2[0], inv)
         n = hb.shape[0] * ROWS
-        dw1, dw2, rest = _gradients(hb.reshape(n, d), eb.reshape(n, ff), ab.reshape(n, ff), gb.reshape(n, d))
+        dw1, dw2, rest, _, _ = _gradients(hb.reshape(n, d), eb.reshape(n, ff), ab.reshape(n, ff), gb.reshape(n, d))
         pp = lax.axis_index('pp')
         own = (pp // 2 + lax.axis_index('dp')) % 2 == pp % 2
         there = [lax.ppermute(rest, ('dp', 'pp'), swap[j]) for j in (0, 1)]

time: 1590 us -> 1570 us (0.987)
  Pallas kernels: 1560 us -> 1540 us
    pallas_call x1, Pallas kernels: 700 us -> 677 us  [_gradients(): pl.pallas_call(_grad_kernel, out_shape=(jax.ShapeDtypeStruct((2, d, ff),...]
where the time goes in v1:
time: 1570 us; the launch traced here: 1560 us
  Pallas kernels  1540 us (98%)
    pallas_call x1, Pallas kernels, _forward_backward(): pl.pallas_call(kern, out_shape=(narrow, wide, wide, wide, narrow, narrow,...  818 us
    pallas_call x1, Pallas kernels, _gradients(): pl.pallas_call(_grad_kernel, out_shape=(jax.ShapeDtypeStruct((2, d, ff),...  677 us
    pallas_call x1, Pallas kernels, _copies(): pl.pallas_call(_copy_kernel, grid=(2, 8), out_shape=(jax.ShapeDtypeStruct...  45.2 us
  transfers between devices with their start and end apart: 4, of which 0 were waited for; matrix products, arithmetic and copies ran while one was open for 0% of the time, Pallas kernels for 3%

profile of v1, /device:TPU:1, one launch (start us, length us, event | category | flops | bytes accessed | tf_op | source)
XLA Modules:
  0.0 1563.3 jit_solution(7204029239500760568)
XLA Ops:
  0.6 818.1 %shard_map.67 = (bf16[64,256,1024]{2,1,0:T(8,128)(2,1)}, bf16[64,256,4096]{2,1,0:T(8,128)(2,1)}, bf16[64,256,4096]{2,1,0:T(8,128)(2,1)}, bf16[64,256,4096]{2,1,0...) custom-call(bf16[32,256,1024]{2,1,0:T(8,128)(2,1)} %bitcast.15, ...), custom_call_target="tpu_custom_call" | custom-call | flops 549755813888 | bytes 671088640 | tf_op jit(solution)/shard_map/pallas_call | solution.py:408
  818.8 677.4 %shard_map.68 = (f32[2,1024,4096]{2,1,0:T(8,128)}, f32[2,4096,1024]{2,1,0:T(8,128)}, f32[1024,512]{1,0:T(8,128)}, f32[256,1024]{1,0:T(8,128)}, f32[256,1024]{1,0:T(8,128)}) custom-call(bf16[16384,1024]{1,0:T(8,128)(2,1)} %bitcast.20, bf16[16384,4096]{1,0:T(8,128)(2,1)} %bitcast.5.e, bf16[16384,4096]{1,0:T(8,128)(2,1)} %bitcast.6.a, bf16[16384,1024]{1,0:T(8,128)(2,1)} %bitcast.21), custom_call_target="tpu_custom_call" | custom-call | flops 274877906944 | bytes 268435456 | tf_op jit(solution)/shard_map/pallas_call | solution.py:600
  1496.2 1.3 collective-permute-start.1
  1497.5 2.0 collective-permute-start
  1499.5 4.9 collective-permute-start.3
  1504.4 3.3 collective-permute-start.2
  1507.7 0.0 copy-start.1
  1507.7 0.0 copy-start
  1507.7 45.2 %shard_map.69 = (f32[2,1024,4096]{2,1,0:T(8,128)}, f32[2,4096,1024]{2,1,0:T(8,128)}) custom-call(f32[2,1024,4096]{2,1,0:T(8,128)} %get-tuple-element.17.a, f32[2,4096,1024]{2,1,0:T(8,128)} %get-tuple-element.18.b), custom_call_target="tpu_custom_call" | custom-call | flops 99999997952 | bytes 134217728 | tf_op jit(solution)/shard_map/pallas_call | solution.py:625
  1552.9 0.0 copy-done.1
  1552.9 0.6 reduce_sum.9
  1554.2 0.0 collective-permute-done.1
  1554.2 0.0 collective-permute-done
  1554.2 0.0 copy-done
  1554.2 4.3 bitcast_dynamic-update-slice_fusion.1
  1558.5 0.0 collective-permute-done.3
  1558.5 0.0 collective-permute-done.2
  1558.5 3.7 bitcast_dynamic-update-slice_fusion
Async XLA Ops:
  1496.2 58.0 %collective-permute-start.1 = (f32[1024,512]{1,0:T(8,128)}, f32[1024,512]{1,0:T(8,128)}, u32[]{:S(2)}, u32[]{:S(2)}) collective-permute-start(f32[1024,512]{1,0:T(8,128)} %get-tuple-element.20), channel_id=1, source_target_pairs={{0,4},{4,1},{2,7},{6,2}} | collective-permute-start | bytes 6291464 | tf_op jit(solution)/shard_map/ppermute | solution.py:654
  1497.5 56.7 %collective-permute-start = (f32[1024,512]{1,0:T(8,128)}, f32[1024,512]{1,0:T(8,128)}, u32[]{:S(2)}, u32[]{:S(2)}) collective-permute-start(f32[1024,512]{1,0:T(8,128)} %get-tuple-element.20), channel_id=1, source_target_pairs={{4,5},{2,3}} | collective-permute-start | bytes 6291464 | tf_op jit(solution)/shard_map/ppermute | solution.py:655
  1499.5 59.0 %collective-permute-start.3 = (f32[1024,512]{1,0:T(8,128)}, f32[1024,512]{1,0:T(8,128)}, u32[]{:S(2)}, u32[]{:S(2)}) collective-permute-start(f32[1024,512]{1,0:T(8,128)} %get-tuple-element.20), channel_id=1, source_target_pairs={{1,4},{5,1},{3,7},{7,2}} | collective-permute-start | bytes 6291464 | tf_op jit(solution)/shard_map/ppermute | solution.py:654
  1504.4 54.1 %collective-permute-start.2 = (f32[1024,512]{1,0:T(8,128)}, f32[1024,512]{1,0:T(8,128)}, u32[]{:S(2)}, u32[]{:S(2)}) collective-permute-start(f32[1024,512]{1,0:T(8,128)} %get-tuple-element.20), channel_id=1, source_target_pairs={{1,0},{7,6}} | collective-permute-start | bytes 6291464 | tf_op jit(solution)/shard_map/ppermute | solution.py:655
  1507.7 45.2 %copy-start.1 = (f32[8,1024]{1,0:T(8,128)S(1)}, f32[8,1024]{1,0:T(8,128)}, u32[]{:S(2)}) copy-start(f32[8,1024]{1,0:T(8,128)} %get-tuple-element.22) | copy-start | bytes 98308
  1507.7 46.5 %copy-start = (f32[1024,512]{1,0:T(8,128)S(1)}, f32[1024,512]{1,0:T(8,128)}, u32[]{:S(2)}) copy-start(f32[1024,512]{1,0:T(8,128)} %get-tuple-element.20) | copy-start | bytes 6291460

commit v2 on v1

--- a/solution.py
+++ b/solution.py
@@ -621,7 +621,8 @@
 
 def _copies(dw1, dw2):
     _, d, ff = dw1.shape
-    specs = [pl.BlockSpec((1, d // 8, ff), lambda j, i: (j, i, 0)), pl.BlockSpec((1, ff // 8, d), lambda j, i: (j, i, 0))]
+    specs = [pl.BlockSpec((1, d // 8, ff - TILE1), lambda j, i: (j, i, 0)),
+             pl.BlockSpec((1, ff // 8, d), lambda j, i: (j, i, 0))]
     return pl.pallas_call(
         _copy_kernel,
         grid=(2, 8),

time: 1570 us -> 1570 us (level)
  no operation moved by 1% of the time
where the time goes in v2:
time: 1570 us; the launch traced here: 1560 us
  Pallas kernels  1540 us (98%)
    pallas_call x1, Pallas kernels, _forward_backward(): pl.pallas_call(kern, out_shape=(narrow, wide, wide, wide, narrow, narrow,...  818 us
    pallas_call x1, Pallas kernels, _gradients(): pl.pallas_call(_grad_kernel, out_shape=(jax.ShapeDtypeStruct((2, d, ff),...  677 us
    pallas_call x1, Pallas kernels, _copies(): pl.pallas_call(_copy_kernel, grid=(2, 8), out_shape=(jax.ShapeDtypeStruct...  43.4 us
  transfers between devices with their start and end apart: 4, of which 0 were waited for; matrix products, arithmetic and copies ran while one was open for 0% of the time, Pallas kernels for 3%

profile of v2, /device:TPU:1, one launch (start us, length us, event | category | flops | bytes accessed | tf_op | source)
XLA Modules:
  0.0 1561.5 jit_solution(18341057772981515424)
XLA Ops:
  0.6 818.1 %shard_map.67 = (bf16[64,256,1024]{2,1,0:T(8,128)(2,1)}, bf16[64,256,4096]{2,1,0:T(8,128)(2,1)}, bf16[64,256,4096]{2,1,0:T(8,128)(2,1)}, bf16[64,256,4096]{2,1,0...) custom-call(bf16[32,256,1024]{2,1,0:T(8,128)(2,1)} %bitcast.15, ...), custom_call_target="tpu_custom_call" | custom-call | flops 549755813888 | bytes 671088640 | tf_op jit(solution)/shard_map/pallas_call | solution.py:408
  818.8 677.4 %shard_map.68 = (f32[2,1024,4096]{2,1,0:T(8,128)}, f32[2,4096,1024]{2,1,0:T(8,128)}, f32[1024,512]{1,0:T(8,128)}, f32[256,1024]{1,0:T(8,128)}, f32[256,1024]{1,0:T(8,128)}) custom-call(bf16[16384,1024]{1,0:T(8,128)(2,1)} %bitcast.20, bf16[16384,4096]{1,0:T(8,128)(2,1)} %bitcast.5.e, bf16[16384,4096]{1,0:T(8,128)(2,1)} %bitcast.6.a, bf16[16384,1024]{1,0:T(8,128)(2,1)} %bitcast.21), custom_call_target="tpu_custom_call" | custom-call | flops 274877906944 | bytes 268435456 | tf_op jit(solution)/shard_map/pallas_call | solution.py:600
  1496.2 1.3 collective-permute-start.1
  1497.5 2.0 collective-permute-start
  1499.5 4.9 collective-permute-start.3
  1504.4 3.3 collective-permute-start.2
  1507.7 0.0 copy-start.1
  1507.7 0.0 copy-start
  1507.7 43.4 %shard_map.69 = (f32[2,1024,4096]{2,1,0:T(8,128)}, f32[2,4096,1024]{2,1,0:T(8,128)}) custom-call(f32[2,1024,4096]{2,1,0:T(8,128)} %get-tuple-element.17.a, f32[2,4096,1024]{2,1,0:T(8,128)} %get-tuple-element.18.b), custom_call_target="tpu_custom_call" | custom-call | flops 99999997952 | bytes 134217728 | tf_op jit(solution)/shard_map/pallas_call | solution.py:626
  1551.1 0.0 copy-done.1
  1551.1 0.6 reduce_sum.9
  1552.3 0.0 collective-permute-done.1
  1552.3 0.0 collective-permute-done
  1552.4 0.0 copy-done
  1552.4 4.3 bitcast_dynamic-update-slice_fusion.1
  1556.7 0.0 collective-permute-done.3
  1556.7 0.0 collective-permute-done.2
  1556.7 3.7 bitcast_dynamic-update-slice_fusion
Async XLA Ops:
  1496.2 56.2 %collective-permute-start.1 = (f32[1024,512]{1,0:T(8,128)}, f32[1024,512]{1,0:T(8,128)}, u32[]{:S(2)}, u32[]{:S(2)}) collective-permute-start(f32[1024,512]{1,0:T(8,128)} %get-tuple-element.20), channel_id=1, source_target_pairs={{0,4},{4,1},{2,7},{6,2}} | collective-permute-start | bytes 6291464 | tf_op jit(solution)/shard_map/ppermute | solution.py:655
  1497.5 54.9 %collective-permute-start = (f32[1024,512]{1,0:T(8,128)}, f32[1024,512]{1,0:T(8,128)}, u32[]{:S(2)}, u32[]{:S(2)}) collective-permute-start(f32[1024,512]{1,0:T(8,128)} %get-tuple-element.20), channel_id=1, source_target_pairs={{4,5},{2,3}} | collective-permute-start | bytes 6291464 | tf_op jit(solution)/shard_map/ppermute | solution.py:656
  1499.5 57.2 %collective-permute-start.3 = (f32[1024,512]{1,0:T(8,128)}, f32[1024,512]{1,0:T(8,128)}, u32[]{:S(2)}, u32[]{:S(2)}) collective-permute-start(f32[1024,512]{1,0:T(8,128)} %get-tuple-element.20), channel_id=1, source_target_pairs={{1,4},{5,1},{3,7},{7,2}} | collective-permute-start | bytes 6291464 | tf_op jit(solution)/shard_map/ppermute | solution.py:655
  1504.4 52.3 %collective-permute-start.2 = (f32[1024,512]{1,0:T(8,128)}, f32[1024,512]{1,0:T(8,128)}, u32[]{:S(2)}, u32[]{:S(2)}) collective-permute-start(f32[1024,512]{1,0:T(8,128)} %get-tuple-element.20), channel_id=1, source_target_pairs={{1,0},{7,6}} | collective-permute-start | bytes 6291464 | tf_op jit(solution)/shard_map/ppermute | solution.py:656
  1507.7 43.4 %copy-start.1 = (f32[8,1024]{1,0:T(8,128)S(1)}, f32[8,1024]{1,0:T(8,128)}, u32[]{:S(2)}) copy-start(f32[8,1024]{1,0:T(8,128)} %get-tuple-element.22) | copy-start | bytes 98308
  1507.7 44.7 %copy-start = (f32[1024,512]{1,0:T(8,128)S(1)}, f32[1024,512]{1,0:T(8,128)}, u32[]{:S(2)}) copy-start(f32[1024,512]{1,0:T(8,128)} %get-tuple-element.20) | copy-start | bytes 6291460
